TPU v7x, 32 devices: a whole 2x2x4 slice. The times are simulated.
32 devices in a mesh: py: 4 (over y, core), pz: 8 (over z, x).
Axes of the slice: x: 2, y: 2, z: 4, core: 2. Of those that a mesh axis runs over, the one named last changes fastest.
Arguments:
- wavefunctions: float32 [2, 8, 128, 128, 128], P(None, None, 'pz', 'py'), may hold values from -6 to 6
- potential: float32 [128, 128, 128], P('pz', 'py'), may hold values from -4 to 4
- cutoff_sq: int32 [1], replicated, may hold values from 2304 to 4096
- locked_mask: int32 [8], replicated, may hold values 0 or 1
Outputs:
- applied: float32 [2, 8, 128, 128, 128], P(None, None, 'pz', 'py')
- rayleigh: float32 [8], replicated
- residual_norm: float32 [8], replicated
All inputs are finite; a program needn't handle non-finite values.
Results may differ from a plain program's by a relative error of at most 0.00005.
Values sent between devices are 32-bit elements; how exact they have to be, the bound alone decides.
A program may use at most 64 MiB of HBM per device.

v0:
```python
import math
import jax
import jax.numpy as jnp
from jax import lax
from jax.sharding import PartitionSpec as P


def make_tables(length, inverse):
    counter = jnp.arange(length, dtype=jnp.int32)
    phase = counter[:, None] * counter[None, :] % length
    angle = 2.0 * math.pi / length * phase.astype(jnp.float32)
    if inverse:
        return (jnp.cos(angle) / length, jnp.sin(angle) / length)
    return (jnp.cos(angle), -jnp.sin(angle))


def transform_axis(field, axis, tables):
    cosines, sines = tables
    letters = "abcdefgh"[: field.ndim - 1]
    place = axis - 1
    source = letters[:place] + "n" + letters[place + 1 :]
    target = letters[:place] + "k" + letters[place + 1 :]
    form = source + ",kn->" + target
    real_part = field[0]
    imag_part = field[1]
    high = lax.Precision.HIGHEST
    out_real = jnp.einsum(form, real_part, cosines, precision=high) - jnp.einsum(
        form, imag_part, sines, precision=high
    )
    out_imag = jnp.einsum(form, real_part, sines, precision=high) + jnp.einsum(
        form, imag_part, cosines, precision=high
    )
    return jnp.stack([out_real, out_imag])


def signed_square(counter, length):
    signed = jnp.where(counter < length // 2, counter, counter - length)
    return signed * signed


def kinetic_table(first_sq, second_sq, third_sq, cutoff_sq, length):
    total = first_sq[:, None, None] + second_sq[None, :, None] + third_sq[None, None, :]
    keep = (total <= cutoff_sq[0]).astype(jnp.float32)
    return 0.5 * (math.pi / length) ** 2 * total.astype(jnp.float32) * keep


def slab_kinetic(field, cutoff_sq, forward, inverse):
    parts, bands, rows_z, rows_y, length = field.shape
    size_y = lax.axis_size("py")
    size_z = lax.axis_size("pz")
    along_x = transform_axis(field, 4, forward)
    flat = jnp.moveaxis(along_x, 1, 3).reshape(parts, rows_z, rows_y, bands * length)
    planes = lax.all_to_all(
        lax.all_to_all(flat, "py", split_axis=3, concat_axis=2, tiled=True),
        "pz",
        split_axis=3,
        concat_axis=1,
        tiled=True,
    )
    width = planes.shape[3]
    start = lax.axis_index("py") * (bands * length // size_y) + lax.axis_index("pz") * width
    column = start + jnp.arange(width, dtype=jnp.int32)
    full_counter = jnp.arange(length, dtype=jnp.int32)
    full_sq = signed_square(full_counter, length)
    kinetic = kinetic_table(
        full_sq, full_sq, signed_square(column % length, length), cutoff_sq, length
    )
    spectrum = transform_axis(transform_axis(planes, 1, forward), 2, forward) * kinetic
    spatial = transform_axis(transform_axis(spectrum, 2, inverse), 1, inverse)
    returned = lax.all_to_all(
        lax.all_to_all(spatial, "py", split_axis=2, concat_axis=3, tiled=True),
        "pz",
        split_axis=1,
        concat_axis=3,
        tiled=True,
    )
    ordered = returned.reshape(parts, rows_z, rows_y, size_z, size_y, width)
    ordered = jnp.swapaxes(ordered, 3, 4).reshape(parts, rows_z, rows_y, bands, length)
    return transform_axis(jnp.moveaxis(ordered, 3, 1), 4, inverse)


def apply_kinetic(field, cutoff_sq, forward, inverse):
    return slab_kinetic(field, cutoff_sq, forward, inverse)


def body(wavefunctions, potential, cutoff_sq, locked_mask):
    length = wavefunctions.shape[4]
    forward = make_tables(length, False)
    inverse = make_tables(length, True)
    blocks = wavefunctions.shape[1] // 4

    def one_block(block, result):
        piece = lax.dynamic_slice_in_dim(wavefunctions, block * 4, 4, 1)
        done = apply_kinetic(piece, cutoff_sq, forward, inverse)
        return lax.dynamic_update_slice_in_dim(result, done, block * 4, 1)

    kinetic_part = lax.fori_loop(0, blocks, one_block, jnp.zeros_like(wavefunctions))
    applied = kinetic_part + potential[None, None] * wavefunctions
    norm_local = jnp.sum(wavefunctions * wavefunctions, axis=(0, 2, 3, 4))
    correlation_local = jnp.sum(wavefunctions * applied, axis=(0, 2, 3, 4))
    norm_sq, correlation = lax.psum((norm_local, correlation_local), ("py", "pz"))
    rayleigh = correlation / norm_sq
    residual = applied - rayleigh[None, :, None, None, None] * wavefunctions
    residual_sq = lax.psum(jnp.sum(residual * residual, axis=(0, 2, 3, 4)), ("py", "pz"))
    residual_norm = jnp.sqrt(residual_sq / norm_sq) * (1.0 - locked_mask.astype(jnp.float32))
    return (applied, rayleigh, residual_norm)


def solution(mesh):
    in_specs = (P(None, None, "pz", "py", None), P("pz", "py", None), P(), P())
    out_specs = (P(None, None, "pz", "py", None), P(), P())
    return jax.shard_map(body, mesh=mesh, in_specs=in_specs, out_specs=out_specs, check_vma=False)
```

profile of v0, /device:TPU:0, one launch (start us, length us, event | category | flops | bytes accessed | tf_op | source)
XLA Modules:
  0.0 693.6 jit_solution(16688748125790381216)
XLA Ops:
  0.6 2.5 broadcast_in_dim.14
  3.2 599.9 %while.18 = (s32[]{:T(128)}, f32[2,8,16,32,128]{4,3,2,1,0:T(8,128)}, f32[2,8,16,32,128]{4,3,2,1,0:T(8,128)}, s32[1]{0:T(128)}, s32[]{:T(128)}, /*index=5*/s32[]{...) while((s32[]{:T(128)}, ...), condition=%wide.region_1.2_spmd.clone.clone, body=%wide.region_0.1_spmd.clone.clone.sunk | while | flops 9676570624 | bytes 232916592 | solution.py:97
  3.2 2.5 fusion.346
  8.1 2.5 fusion.347
  10.6 2.5 fusion.345
  13.3 7.5 %copy.142 = f32[2,16,32,4,128]{2,1,0,4,3:T(8,128)} copy(f32[2,16,32,4,128]{4,2,1,3,0:T(8,128)S(1)} %maximum_bitcast_fusion.2) | data formatting | bytes 4194304 | tf_op jit(solution)/shard_map/while/body/eval_jaxpr/reshape | solution.py:52
  20.7 6.1 reshape.143
  26.9 30.2 %all_to_all.204 = f32[4,1,131072]{2,1,0:T(1,128)} all-to-all(f32[4,1,131072]{2,1,0:T(1,128)S(1)} %reshape.143), channel_id=1, replica_groups=mesh['py'=4,'pz'=8] {'py'}, dimensions={0} | all-to-all | bytes 4194304 | tf_op jit(solution)/shard_map/while/body/eval_jaxpr/all_to_all | solution.py:54
  57.6 7.7 %reduce.4 = f32[4,131072]{1,0:T(4,128)S(1)} reduce(f32[4,1,131072]{2,1,0:T(1,128)} %all_to_all.204, f32[]{:T(128)} %broadcast.656), dimensions={1}, to_apply=%all_to_all.178.reduce_sub_computation | reduce | bytes 4194308 | tf_op jit(solution)/shard_map/while/body/eval_jaxpr/all_to_all | solution.py:54
  65.3 6.1 reshape.144
  71.4 5.2 copy.143
  78.2 3.1 copy.145
  81.3 6.9 all-to-all-start.1
  89.3 46.3 %all-to-all-done.1 = f32[2,16,128,128]{2,1,0,3:T(8,128)S(1)} async-done(((f32[2,16,128,128]{2,1,0,3:T(8,128)}), f32[2,16,128,128]{2,1,0,3:T(8,128)S(1)}, u32[]{:S(2)}, u32[]{:S(2)}) %all-to-all-start.1) | async-done | bytes 2097184 | tf_op jit(solution)/shard_map/while/body/eval_jaxpr/all_to_all | solution.py:53
  170.9 28.1 %all_to_all.205 = f32[2,128,128,16]{1,3,0,2:T(8,128)S(1)} all-to-all(f32[2,128,128,16]{1,3,0,2:T(8,128)S(1)} %copy.151), channel_id=1, replica_groups=mesh['py'=4,'pz'=8] {'py'}, dimensions={2} | all-to-all | bytes 4194304 | tf_op jit(solution)/shard_map/while/body/eval_jaxpr/all_to_all | solution.py:71
  199.3 4.5 copy.153
  203.8 7.2 %reshape.145 = f32[8,1,65536]{2,1,0:T(1,128)} reshape(f32[128,2,32,64]{3,2,1,0:T(8,128)} %bitcast.327) | data formatting | bytes 4194304 | tf_op jit(solution)/shard_map/while
  211.0 3.9 all-to-all-start.3
  214.9 48.0 %all-to-all-done.3 = f32[8,1,65536]{2,1,0:T(1,128)S(1)} async-done(((f32[8,1,65536]{2,1,0:T(1,128)}), f32[8,1,65536]{2,1,0:T(1,128)S(1)}, u32[]{:S(2)}, u32[]{:S(2)}) %all-to-all-start.3) | async-done | bytes 2097184 | tf_op jit(solution)/shard_map/while/body/eval_jaxpr/all_to_all | solution.py:70
  264.8 7.2 %reduce.5 = f32[8,65536]{1,0:T(8,128)S(1)} reduce(f32[8,1,65536]{2,1,0:T(1,128)} %copy-done, f32[]{:T(128)} %broadcast.657), dimensions={1}, to_apply=%all_to_all.189.reduce_sub_computation | reduce | bytes 4194308 | tf_op jit(solution)/shard_map/while/body/eval_jaxpr/all_to_all | solution.py:70
  272.0 3.6 reshape.146
  275.6 7.0 %copy.154 = f32[2,16,32,8,64]{2,4,3,1,0:T(8,128)} copy(f32[2,16,32,8,64]{4,2,0,1,3:T(8,128)} %bitcast.326) | data formatting | bytes 4194304 | tf_op jit(solution)/shard_map/while/body/eval_jaxpr/all_to_all | solution.py:70
  282.6 7.9 %copy.155 = f32[2,16,32,4,8,16]{2,5,4,3,1,0:T(8,128)} copy(f32[2,16,32,4,8,16]{2,5,3,4,1,0:T(8,128)} %bitcast.320) | data formatting | bytes 4194304 | tf_op jit(solution)/shard_map/while/body/eval_jaxpr/transpose | solution.py:78
  290.5 5.6 copy.156
  308.4 2.5 fusion.347
  313.5 7.5 %copy.142 = f32[2,16,32,4,128]{2,1,0,4,3:T(8,128)} copy(f32[2,16,32,4,128]{4,2,1,3,0:T(8,128)S(1)} %maximum_bitcast_fusion.2) | data formatting | bytes 4194304 | tf_op jit(solution)/shard_map/while/body/eval_jaxpr/reshape | solution.py:52
  321.0 6.1 reshape.143
  327.2 29.1 %all_to_all.204 = f32[4,1,131072]{2,1,0:T(1,128)} all-to-all(f32[4,1,131072]{2,1,0:T(1,128)S(1)} %reshape.143), channel_id=1, replica_groups=mesh['py'=4,'pz'=8] {'py'}, dimensions={0} | all-to-all | bytes 4194304 | tf_op jit(solution)/shard_map/while/body/eval_jaxpr/all_to_all | solution.py:54
  356.8 7.7 %reduce.4 = f32[4,131072]{1,0:T(4,128)S(1)} reduce(f32[4,1,131072]{2,1,0:T(1,128)} %all_to_all.204, f32[]{:T(128)} %broadcast.656), dimensions={1}, to_apply=%all_to_all.178.reduce_sub_computation | reduce | bytes 4194308 | tf_op jit(solution)/shard_map/while/body/eval_jaxpr/all_to_all | solution.py:54
  364.5 6.1 reshape.144
  370.6 5.2 copy.143
  377.5 3.1 copy.145
  380.5 4.0 all-to-all-start.1
  385.6 46.7 %all-to-all-done.1 = f32[2,16,128,128]{2,1,0,3:T(8,128)S(1)} async-done(((f32[2,16,128,128]{2,1,0,3:T(8,128)}), f32[2,16,128,128]{2,1,0,3:T(8,128)S(1)}, u32[]{:S(2)}, u32[]{:S(2)}) %all-to-all-start.1) | async-done | bytes 2097184 | tf_op jit(solution)/shard_map/while/body/eval_jaxpr/all_to_all | solution.py:53
  467.6 28.1 %all_to_all.205 = f32[2,128,128,16]{1,3,0,2:T(8,128)S(1)} all-to-all(f32[2,128,128,16]{1,3,0,2:T(8,128)S(1)} %copy.151), channel_id=1, replica_groups=mesh['py'=4,'pz'=8] {'py'}, dimensions={2} | all-to-all | bytes 4194304 | tf_op jit(solution)/shard_map/while/body/eval_jaxpr/all_to_all | solution.py:71
  496.0 4.5 copy.153
  500.5 7.2 %reshape.145 = f32[8,1,65536]{2,1,0:T(1,128)} reshape(f32[128,2,32,64]{3,2,1,0:T(8,128)} %bitcast.327) | data formatting | bytes 4194304 | tf_op jit(solution)/shard_map/while
  507.7 3.9 all-to-all-start.3
  511.6 48.0 %all-to-all-done.3 = f32[8,1,65536]{2,1,0:T(1,128)S(1)} async-done(((f32[8,1,65536]{2,1,0:T(1,128)}), f32[8,1,65536]{2,1,0:T(1,128)S(1)}, u32[]{:S(2)}, u32[]{:S(2)}) %all-to-all-start.3) | async-done | bytes 2097184 | tf_op jit(solution)/shard_map/while/body/eval_jaxpr/all_to_all | solution.py:70
  561.5 7.2 %reduce.5 = f32[8,65536]{1,0:T(8,128)S(1)} reduce(f32[8,1,65536]{2,1,0:T(1,128)} %copy-done, f32[]{:T(128)} %broadcast.657), dimensions={1}, to_apply=%all_to_all.189.reduce_sub_computation | reduce | bytes 4194308 | tf_op jit(solution)/shard_map/while/body/eval_jaxpr/all_to_all | solution.py:70
  568.7 3.6 reshape.146
  572.3 7.0 %copy.154 = f32[2,16,32,8,64]{2,4,3,1,0:T(8,128)} copy(f32[2,16,32,8,64]{4,2,0,1,3:T(8,128)} %bitcast.326) | data formatting | bytes 4194304 | tf_op jit(solution)/shard_map/while/body/eval_jaxpr/all_to_all | solution.py:70
  579.3 7.9 %copy.155 = f32[2,16,32,4,8,16]{2,5,4,3,1,0:T(8,128)} copy(f32[2,16,32,4,8,16]{2,5,3,4,1,0:T(8,128)} %bitcast.320) | data formatting | bytes 4194304 | tf_op jit(solution)/shard_map/while/body/eval_jaxpr/transpose | solution.py:78
  587.2 5.6 copy.156
  603.1 6.5 multiply_reduce_fusion.1
  609.6 37.5 %all-reduce = (f32[8]{0:T(128)S(1)}, f32[8]{0:T(128)S(1)}) all-reduce(f32[8]{0:T(128)S(1)} %get-tuple-element.349, f32[8]{0:T(128)S(1)} %get-tuple-element.348), channel_id=1, replica_groups=mesh['py'=4,'pz'=8] {'py','pz'}, use_global_device_ids=true, to_apply=%region_3.4 | all-reduce | flops 16 | bytes 128 | tf_op jit(solution)/shard_map/psum | solution.py:101
  647.2 4.2 multiply_reduce_fusion
  651.4 41.5 %psum.23 = f32[8]{0:T(128)S(1)} all-reduce(f32[8]{0:T(128)S(1)} %multiply_reduce_fusion), channel_id=1, replica_groups=mesh['py'=4,'pz'=8] {'py','pz'}, use_global_device_ids=true, to_apply=%region_7.8 | all-reduce | flops 8 | bytes 64 | tf_op jit(solution)/shard_map/psum | solution.py:104
  (106 shorter events, 105.8 us)
Async XLA Ops:
  3.2 599.9 %copy-start.4 = (f32[16,32,128]{2,1,0:T(8,128)S(1)}, f32[16,32,128]{2,1,0:T(8,128)}, u32[]{:S(2)}) copy-start(f32[16,32,128]{2,1,0:T(8,128)} %param.7) | copy-start | bytes 786436
  81.3 54.2 %all-to-all-start.1 = ((f32[2,16,128,128]{2,1,0,3:T(8,128)}), f32[2,16,128,128]{2,1,0,3:T(8,128)S(1)}, u32[]{:S(2)}, u32[]{:S(2)}) async-start(f32[2,16,128,128]{2,1,0,3:T(8,128)} %copy.145), calls=%async_computation.1 | async-start | bytes 4194304 | tf_op jit(solution)/shard_map/while/body/eval_jaxpr/all_to_all | solution.py:53
  138.5 3.5 copy-start.1
  211.0 51.9 %all-to-all-start.3 = ((f32[8,1,65536]{2,1,0:T(1,128)}), f32[8,1,65536]{2,1,0:T(1,128)S(1)}, u32[]{:S(2)}, u32[]{:S(2)}) async-start(f32[8,1,65536]{2,1,0:T(1,128)} %reshape.145), calls=%async_computation.3 | async-start | bytes 4194304 | tf_op jit(solution)/shard_map/while/body/eval_jaxpr/all_to_all | solution.py:70
  262.9 1.4 copy-start
  298.6 2.5 copy-start.2
  301.3 2.0 copy-start.3
  380.5 51.7 %all-to-all-start.1 = ((f32[2,16,128,128]{2,1,0,3:T(8,128)}), f32[2,16,128,128]{2,1,0,3:T(8,128)S(1)}, u32[]{:S(2)}, u32[]{:S(2)}) async-start(f32[2,16,128,128]{2,1,0,3:T(8,128)} %copy.145), calls=%async_computation.1 | async-start | bytes 4194304 | tf_op jit(solution)/shard_map/while/body/eval_jaxpr/all_to_all | solution.py:53
  435.2 3.5 copy-start.1
  507.7 51.9 %all-to-all-start.3 = ((f32[8,1,65536]{2,1,0:T(1,128)}), f32[8,1,65536]{2,1,0:T(1,128)S(1)}, u32[]{:S(2)}, u32[]{:S(2)}) async-start(f32[8,1,65536]{2,1,0:T(1,128)} %reshape.145), calls=%async_computation.3 | async-start | bytes 4194304 | tf_op jit(solution)/shard_map/while/body/eval_jaxpr/all_to_all | solution.py:70
  559.6 1.4 copy-start
  595.2 2.5 copy-start.2
  598.0 2.0 copy-start.3
  647.1 4.2 copy-start.5
  647.2 45.7 %copy-start.6 = (s32[8]{0:T(128)S(1)}, s32[8]{0:T(128)}, u32[]{:S(2)}) copy-start(s32[8]{0:T(128)} %param.9) | copy-start | bytes 100
where the time goes:
time: 697 us; the launch traced here: 694 us
  blocking collectives  195 us (28%)
  waiting for transfers between devices  189 us (27%)
  local copies, waits for them, and re-layouts  156 us (22%)
  matrix products  85.4 us (12%)
  other arithmetic  44.8 us (6%)
  starting transfers between devices  18.7 us (3%)
    all_to_all x2, waiting for transfers between devices, slab_kinetic(): lax.all_to_all(lax.all_to_all(spatial, 'py', split_axis=2, concat_axis=3,...  96 us
    all_to_all x2, waiting for transfers between devices, slab_kinetic(): lax.all_to_all(lax.all_to_all(flat, 'py', split_axis=3, concat_axis=2, ti...  92.9 us
    all_to_all x2, blocking collectives, slab_kinetic(): lax.all_to_all(flat, 'py', split_axis=3, concat_axis=2, tiled=True)  59.3 us
    all_to_all x2, blocking collectives, slab_kinetic(): lax.all_to_all(spatial, 'py', split_axis=2, concat_axis=3, tiled=True)  56.3 us
    while x24, local copies, waits for them, and re-layouts  52.9 us
    psum x1, blocking collectives, body(): lax.psum(jnp.sum(residual * residual, axis=(0, 2, 3, 4)), ('py', 'pz'))  41.5 us
    psum x1, blocking collectives, body(): lax.psum((norm_local, correlation_local), ('py', 'pz'))  37.5 us
    dot_general x12, matrix products, transform_axis(): jnp.einsum(form, imag_part, sines, precision=high)  22.5 us
  transfers between devices with their start and end apart: 4, of which 4 were waited for; matrix products, arithmetic and copies ran while one was open for 0% of the time, Pallas kernels for 0%

commit v1 on v0

--- a/solution.py
+++ b/solution.py
@@ -68,7 +68,10 @@
     spectrum = transform_axis(transform_axis(planes, 1, forward), 2, forward) * kinetic
     spatial = transform_axis(transform_axis(spectrum, 2, inverse), 1, inverse)
     returned = lax.all_to_all(
-        lax.all_to_all(spatial, "py", split_axis=2, concat_axis=3, tiled=True),
+        jnp.concatenate(
+            lax.all_to_all(jnp.stack(jnp.split(spatial, lax.axis_size("py"), axis=2)), "py", 0, 0),
+            axis=3,
+        ),
         "pz",
         split_axis=1,
         concat_axis=3,

time: 697 us -> 697 us (level)
    reshape x0 -> x4, local copies, waits for them, and re-layouts: none -> 11.4 us  [slab_kinetic(): jnp.concatenate(lax.all_to_all(jnp.stack(jnp.split(spatial, lax.axis_size...]
    all_to_all x8 -> x4, local copies, waits for them, and re-layouts: 24.5 us -> 15 us  [slab_kinetic(): lax.all_to_all(jnp.concatenate(lax.all_to_all(jnp.stack(jnp.split(spatial...]
where the time goes in v1:
time: 697 us; the launch traced here: 694 us
  blocking collectives  195 us (28%)
  waiting for transfers between devices  189 us (27%)
  local copies, waits for them, and re-layouts  156 us (22%)
  matrix products  85.3 us (12%)
  other arithmetic  45.2 us (6%)
  starting transfers between devices  18.7 us (3%)
    all_to_all x2, waiting for transfers between devices, slab_kinetic(): lax.all_to_all(jnp.concatenate(lax.all_to_all(jnp.stack(jnp.split(spatial...  96 us
    all_to_all x2, waiting for transfers between devices, slab_kinetic(): lax.all_to_all(lax.all_to_all(flat, 'py', split_axis=3, concat_axis=2, ti...  92.9 us
    all_to_all x2, blocking collectives, slab_kinetic(): lax.all_to_all(flat, 'py', split_axis=3, concat_axis=2, tiled=True)  59.3 us
    all_to_all x2, blocking collectives, slab_kinetic(): lax.all_to_all(jnp.stack(jnp.split(spatial, lax.axis_size('py'), axis=2))...  56.3 us
    while x24, local copies, waits for them, and re-layouts  52.9 us
    psum x1, blocking collectives, body(): lax.psum(jnp.sum(residual * residual, axis=(0, 2, 3, 4)), ('py', 'pz'))  41.5 us
    psum x1, blocking collectives, body(): lax.psum((norm_local, correlation_local), ('py', 'pz'))  37.5 us
    dot_general x12, matrix products, transform_axis(): jnp.einsum(form, imag_part, sines, precision=high)  22.5 us
  transfers between devices with their start and end apart: 4, of which 4 were waited for; matrix products, arithmetic and copies ran while one was open for 0% of the time, Pallas kernels for 0%

profile of v1, /device:TPU:0, one launch (start us, length us, event | category | flops | bytes accessed | tf_op | source)
XLA Modules:
  0.0 693.5 jit_solution(15916022973731821663)
XLA Ops:
  0.6 2.5 broadcast_in_dim.14
  3.2 599.8 %while.18 = (s32[]{:T(128)}, f32[2,8,16,32,128]{4,3,2,1,0:T(8,128)}, f32[2,8,16,32,128]{4,3,2,1,0:T(8,128)}, s32[1]{0:T(128)}, s32[]{:T(128)}, /*index=5*/s32[]{...) while((s32[]{:T(128)}, ...), condition=%wide.region_1.2_spmd.clone.clone, body=%wide.region_0.1_spmd.clone.clone.sunk | while | flops 9678143488 | bytes 232916592 | solution.py:100
  3.2 2.5 fusion.354
  8.1 2.5 fusion.355
  10.6 2.5 fusion.353
  13.3 7.5 %copy.138 = f32[2,16,32,4,128]{2,1,0,4,3:T(8,128)} copy(f32[2,16,32,4,128]{4,2,1,3,0:T(8,128)S(1)} %maximum_bitcast_fusion.2) | data formatting | bytes 4194304 | tf_op jit(solution)/shard_map/while/body/eval_jaxpr/reshape | solution.py:52
  20.7 6.1 reshape.169
  26.9 30.2 %all_to_all.164 = f32[4,1,131072]{2,1,0:T(1,128)} all-to-all(f32[4,1,131072]{2,1,0:T(1,128)S(1)} %reshape.169), channel_id=1, replica_groups=mesh['py'=4,'pz'=8] {'py'}, dimensions={0} | all-to-all | bytes 4194304 | tf_op jit(solution)/shard_map/while/body/eval_jaxpr/all_to_all | solution.py:54
  57.6 7.7 %reduce.4 = f32[4,131072]{1,0:T(4,128)S(1)} reduce(f32[4,1,131072]{2,1,0:T(1,128)} %all_to_all.164, f32[]{:T(128)} %broadcast.656), dimensions={1}, to_apply=%all_to_all.141.reduce_sub_computation | reduce | bytes 4194308 | tf_op jit(solution)/shard_map/while/body/eval_jaxpr/all_to_all | solution.py:54
  65.3 6.1 reshape.170
  71.4 5.2 copy.139
  78.2 3.1 copy.141
  81.3 6.9 all-to-all-start.1
  89.3 46.3 %all-to-all-done.1 = f32[2,16,128,128]{2,1,0,3:T(8,128)S(1)} async-done(((f32[2,16,128,128]{2,1,0,3:T(8,128)}), f32[2,16,128,128]{2,1,0,3:T(8,128)S(1)}, u32[]{:S(2)}, u32[]{:S(2)}) %all-to-all-start.1) | async-done | bytes 2097184 | tf_op jit(solution)/shard_map/while/body/eval_jaxpr/all_to_all | solution.py:53
  169.9 28.1 %all_to_all.165 = f32[4,2,128,32,16]{2,3,4,1,0:T(8,128)S(1)} all-to-all(f32[4,2,128,32,16]{2,3,4,1,0:T(8,128)S(1)} %pad_maximum_fusion.3), channel_id=1, replica_groups=mesh['py'=4,'pz'=8] {'py'}, dimensions={0} | all-to-all | bytes 4194304 | tf_op jit(solution)/shard_map/while/body/eval_jaxpr/all_to_all | solution.py:72
  199.2 4.5 copy.148
  203.8 7.2 %reshape.171 = f32[8,1,65536]{2,1,0:T(1,128)} reshape(f32[128,2,32,64]{3,2,1,0:T(8,128)} %bitcast.335) | data formatting | bytes 4194304 | tf_op jit(solution)/shard_map/while
  210.9 3.9 all-to-all-start.3
  214.9 48.0 %all-to-all-done.3 = f32[8,1,65536]{2,1,0:T(1,128)S(1)} async-done(((f32[8,1,65536]{2,1,0:T(1,128)}), f32[8,1,65536]{2,1,0:T(1,128)S(1)}, u32[]{:S(2)}, u32[]{:S(2)}) %all-to-all-start.3) | async-done | bytes 2097184 | tf_op jit(solution)/shard_map/while/body/eval_jaxpr/all_to_all | solution.py:70
  264.7 7.2 %reduce.5 = f32[8,65536]{1,0:T(8,128)S(1)} reduce(f32[8,1,65536]{2,1,0:T(1,128)} %copy-done, f32[]{:T(128)} %broadcast.657), dimensions={1}, to_apply=%all_to_all.149.reduce_sub_computation | reduce | bytes 4194308 | tf_op jit(solution)/shard_map/while/body/eval_jaxpr/all_to_all | solution.py:70
  272.0 3.6 reshape.172
  275.6 7.0 %copy.149 = f32[2,16,32,8,64]{2,4,3,1,0:T(8,128)} copy(f32[2,16,32,8,64]{4,2,0,1,3:T(8,128)} %bitcast.334) | data formatting | bytes 4194304 | tf_op jit(solution)/shard_map/while/body/eval_jaxpr/all_to_all | solution.py:70
  282.6 7.9 %copy.150 = f32[2,16,32,4,8,16]{2,5,4,3,1,0:T(8,128)} copy(f32[2,16,32,4,8,16]{2,5,3,4,1,0:T(8,128)} %bitcast.328) | data formatting | bytes 4194304 | tf_op jit(solution)/shard_map/while/body/eval_jaxpr/transpose | solution.py:81
  290.5 5.6 copy.151
  308.4 2.5 fusion.355
  313.5 7.5 %copy.138 = f32[2,16,32,4,128]{2,1,0,4,3:T(8,128)} copy(f32[2,16,32,4,128]{4,2,1,3,0:T(8,128)S(1)} %maximum_bitcast_fusion.2) | data formatting | bytes 4194304 | tf_op jit(solution)/shard_map/while/body/eval_jaxpr/reshape | solution.py:52
  321.0 6.1 reshape.169
  327.1 29.1 %all_to_all.164 = f32[4,1,131072]{2,1,0:T(1,128)} all-to-all(f32[4,1,131072]{2,1,0:T(1,128)S(1)} %reshape.169), channel_id=1, replica_groups=mesh['py'=4,'pz'=8] {'py'}, dimensions={0} | all-to-all | bytes 4194304 | tf_op jit(solution)/shard_map/while/body/eval_jaxpr/all_to_all | solution.py:54
  356.7 7.7 %reduce.4 = f32[4,131072]{1,0:T(4,128)S(1)} reduce(f32[4,1,131072]{2,1,0:T(1,128)} %all_to_all.164, f32[]{:T(128)} %broadcast.656), dimensions={1}, to_apply=%all_to_all.141.reduce_sub_computation | reduce | bytes 4194308 | tf_op jit(solution)/shard_map/while/body/eval_jaxpr/all_to_all | solution.py:54
  364.4 6.1 reshape.170
  370.6 5.2 copy.139
  377.4 3.1 copy.141
  380.5 4.0 all-to-all-start.1
  385.5 46.7 %all-to-all-done.1 = f32[2,16,128,128]{2,1,0,3:T(8,128)S(1)} async-done(((f32[2,16,128,128]{2,1,0,3:T(8,128)}), f32[2,16,128,128]{2,1,0,3:T(8,128)S(1)}, u32[]{:S(2)}, u32[]{:S(2)}) %all-to-all-start.1) | async-done | bytes 2097184 | tf_op jit(solution)/shard_map/while/body/eval_jaxpr/all_to_all | solution.py:53
  466.5 28.1 %all_to_all.165 = f32[4,2,128,32,16]{2,3,4,1,0:T(8,128)S(1)} all-to-all(f32[4,2,128,32,16]{2,3,4,1,0:T(8,128)S(1)} %pad_maximum_fusion.3), channel_id=1, replica_groups=mesh['py'=4,'pz'=8] {'py'}, dimensions={0} | all-to-all | bytes 4194304 | tf_op jit(solution)/shard_map/while/body/eval_jaxpr/all_to_all | solution.py:72
  495.9 4.5 copy.148
  500.4 7.2 %reshape.171 = f32[8,1,65536]{2,1,0:T(1,128)} reshape(f32[128,2,32,64]{3,2,1,0:T(8,128)} %bitcast.335) | data formatting | bytes 4194304 | tf_op jit(solution)/shard_map/while
  507.6 3.9 all-to-all-start.3
  511.5 48.0 %all-to-all-done.3 = f32[8,1,65536]{2,1,0:T(1,128)S(1)} async-done(((f32[8,1,65536]{2,1,0:T(1,128)}), f32[8,1,65536]{2,1,0:T(1,128)S(1)}, u32[]{:S(2)}, u32[]{:S(2)}) %all-to-all-start.3) | async-done | bytes 2097184 | tf_op jit(solution)/shard_map/while/body/eval_jaxpr/all_to_all | solution.py:70
  561.3 7.2 %reduce.5 = f32[8,65536]{1,0:T(8,128)S(1)} reduce(f32[8,1,65536]{2,1,0:T(1,128)} %copy-done, f32[]{:T(128)} %broadcast.657), dimensions={1}, to_apply=%all_to_all.149.reduce_sub_computation | reduce | bytes 4194308 | tf_op jit(solution)/shard_map/while/body/eval_jaxpr/all_to_all | solution.py:70
  568.6 3.6 reshape.172
  572.2 7.0 %copy.149 = f32[2,16,32,8,64]{2,4,3,1,0:T(8,128)} copy(f32[2,16,32,8,64]{4,2,0,1,3:T(8,128)} %bitcast.334) | data formatting | bytes 4194304 | tf_op jit(solution)/shard_map/while/body/eval_jaxpr/all_to_all | solution.py:70
  579.2 7.9 %copy.150 = f32[2,16,32,4,8,16]{2,5,4,3,1,0:T(8,128)} copy(f32[2,16,32,4,8,16]{2,5,3,4,1,0:T(8,128)} %bitcast.328) | data formatting | bytes 4194304 | tf_op jit(solution)/shard_map/while/body/eval_jaxpr/transpose | solution.py:81
  587.1 5.6 copy.151
  603.0 6.5 multiply_reduce_fusion.1
  609.5 37.5 %all-reduce = (f32[8]{0:T(128)S(1)}, f32[8]{0:T(128)S(1)}) all-reduce(f32[8]{0:T(128)S(1)} %get-tuple-element.349, f32[8]{0:T(128)S(1)} %get-tuple-element.348), channel_id=1, replica_groups=mesh['py'=4,'pz'=8] {'py','pz'}, use_global_device_ids=true, to_apply=%region_3.4 | all-reduce | flops 16 | bytes 128 | tf_op jit(solution)/shard_map/psum | solution.py:104
  647.0 4.2 multiply_reduce_fusion
  651.3 41.5 %psum.23 = f32[8]{0:T(128)S(1)} all-reduce(f32[8]{0:T(128)S(1)} %multiply_reduce_fusion), channel_id=1, replica_groups=mesh['py'=4,'pz'=8] {'py','pz'}, use_global_device_ids=true, to_apply=%region_7.8 | all-reduce | flops 8 | bytes 64 | tf_op jit(solution)/shard_map/psum | solution.py:107
  (106 shorter events, 105.7 us)
Async XLA Ops:
  3.2 599.8 %copy-start.4 = (f32[16,32,128]{2,1,0:T(8,128)S(1)}, f32[16,32,128]{2,1,0:T(8,128)}, u32[]{:S(2)}) copy-start(f32[16,32,128]{2,1,0:T(8,128)} %param.7) | copy-start | bytes 786436
  81.3 54.2 %all-to-all-start.1 = ((f32[2,16,128,128]{2,1,0,3:T(8,128)}), f32[2,16,128,128]{2,1,0,3:T(8,128)S(1)}, u32[]{:S(2)}, u32[]{:S(2)}) async-start(f32[2,16,128,128]{2,1,0,3:T(8,128)} %copy.141), calls=%async_computation.1 | async-start | bytes 4194304 | tf_op jit(solution)/shard_map/while/body/eval_jaxpr/all_to_all | solution.py:53
  138.5 3.5 copy-start.1
  210.9 51.9 %all-to-all-start.3 = ((f32[8,1,65536]{2,1,0:T(1,128)}), f32[8,1,65536]{2,1,0:T(1,128)S(1)}, u32[]{:S(2)}, u32[]{:S(2)}) async-start(f32[8,1,65536]{2,1,0:T(1,128)} %reshape.171), calls=%async_computation.3 | async-start | bytes 4194304 | tf_op jit(solution)/shard_map/while/body/eval_jaxpr/all_to_all | solution.py:70
  262.9 1.4 copy-start
  298.5 2.5 copy-start.2
  301.3 2.0 copy-start.3
  380.5 51.7 %all-to-all-start.1 = ((f32[2,16,128,128]{2,1,0,3:T(8,128)}), f32[2,16,128,128]{2,1,0,3:T(8,128)S(1)}, u32[]{:S(2)}, u32[]{:S(2)}) async-start(f32[2,16,128,128]{2,1,0,3:T(8,128)} %copy.141), calls=%async_computation.1 | async-start | bytes 4194304 | tf_op jit(solution)/shard_map/while/body/eval_jaxpr/all_to_all | solution.py:53
  435.1 3.5 copy-start.1
  507.6 51.9 %all-to-all-start.3 = ((f32[8,1,65536]{2,1,0:T(1,128)}), f32[8,1,65536]{2,1,0:T(1,128)S(1)}, u32[]{:S(2)}, u32[]{:S(2)}) async-start(f32[8,1,65536]{2,1,0:T(1,128)} %reshape.171), calls=%async_computation.3 | async-start | bytes 4194304 | tf_op jit(solution)/shard_map/while/body/eval_jaxpr/all_to_all | solution.py:70
  559.5 1.4 copy-start
  595.1 2.5 copy-start.2
  597.9 2.0 copy-start.3
  647.0 4.2 copy-start.5
  647.0 45.7 %copy-start.6 = (s32[8]{0:T(128)S(1)}, s32[8]{0:T(128)}, u32[]{:S(2)}) copy-start(s32[8]{0:T(128)} %param.9) | copy-start | bytes 100
